TPU v7x, 16 devices: a whole 2x2x2 slice. The times are simulated.
16 devices in a mesh: dp: 1, tp: 16 (over x, y, z, core).
Axes of the slice: x: 2, y: 2, z: 2, core: 2. Of those that a mesh axis runs over, the one named last changes fastest.
Arguments:
- x: bfloat16 [2048, 8192], P(('dp', 'tp'))
- dy: bfloat16 [2048, 8192], P(('dp', 'tp'))
- gate: bfloat16 [2048, 49152], P('dp', 'tp')
- up: bfloat16 [2048, 49152], P('dp', 'tp')
- w_gate: bfloat16 [8192, 49152], P(None, 'tp')
- w_up: bfloat16 [8192, 49152], P(None, 'tp')
- w_down: bfloat16 [49152, 8192], P('tp')
Outputs:
- output 1: bfloat16 [2048, 8192], P(('dp', 'tp'))
- output 2: bfloat16 [8192, 49152], P('dp', 'tp')
- output 3: bfloat16 [8192, 49152], P('dp', 'tp')
- output 4: bfloat16 [49152, 8192], P(('dp', 'tp'))
All inputs are finite; a program needn't handle non-finite values.
Results may differ from a plain program's by a relative error of at most 0.012.
Values are sent between devices in bfloat16 or wider.
A program may use at most 2 GiB of HBM per device.

v0:
```python
import jax
import jax.numpy as jnp


def act(gate, up):
    return jax.nn.silu(gate) * up


def solution(mesh):
    def step(x, dy, gate, up, w_gate, w_up, w_down):
        hidden, back = jax.vjp(act, gate.astype(jnp.float32), up.astype(jnp.float32))
        d_hidden = jnp.dot(dy, w_down.T, preferred_element_type=jnp.float32)
        d_gate, d_up = (g.astype(jnp.bfloat16) for g in back(d_hidden))
        dx = jnp.dot(d_gate, w_gate.T) + jnp.dot(d_up, w_up.T)
        groups = mesh.shape["dp"]

        def by_group(a, b):
            a, b = (t.reshape(groups, -1, t.shape[-1]) for t in (a, b))
            product = jnp.einsum("gta,gtb->gab", a, b, preferred_element_type=jnp.float32)
            return product.astype(jnp.bfloat16).reshape(-1, b.shape[-1])

        return dx, by_group(x, d_gate), by_group(x, d_up), by_group(hidden.astype(jnp.bfloat16), dy)

    return step
```

profile of v0, /device:TPU:1, one launch (start us, length us, event | category | flops | bytes accessed | tf_op | source)
XLA Modules:
  0.0 1691.4 jit_solution(12702790263890746)
XLA Ops:
  8.7 135.2 %all-gather.7.cloned.1.call-done = bf16[2048,8192]{1,0:T(8,128)(2,1)} async-done(((bf16[128,8192]{1,0:T(8,128)(2,1)}), bf16[2048,8192]{1,0:T(8,128)(2,1)}) %all-gather.7.cloned.1.call-update) | async-done | bytes 33554448 | tf_op args[1]
  143.9 128.7 %fusion.38 = (bf16[2048,3072]{1,0:T(8,128)(2,1)}, bf16[2048,3072]{1,0:T(8,128)(2,1)}) fusion(bf16[2048,3072]{1,0:T(8,128)(2,1)} %param.7, bf16[2048,3072]{1,0:T(8,128)(2,1)} %param.6, bf16[2048,8192]{1,0:T(8,128)(2,1)} %all-gather.7.cloned.1.call-done, bf16[3072,8192]{1,0:T(8,128)(2,1)} %param.5), kind=kOutput, calls=%fused_computation.63 | convolution fusion | flops 103179878400 | bytes 134217728 | tf_op jit(solution)/dot_general | solution.py:12
  272.6 460.0 %while.4 = (bf16[2048,3072]{1,0:T(8,128)(2,1)}, bf16[8192,3072]{1,0:T(8,128)(2,1)}, bf16[128,8192]{1,0:T(8,128)(2,1)}, bf16[128,8192]{1,0:T(8,128)(2,1)}, u32[]{...) while((bf16[2048,3072]{1,0:T(8,128)(2,1)}, ...), condition=%wide.windowed_dot_general_cond_rs.clone, body=%wide.windowed_dot_general_body_rs.clone.sunk | while | flops 25782386688 | bytes 209715840 | solution.py:14
  277.3 22.0 %fusion.71 = bf16[2,128,8192]{2,1,0:T(8,128)(2,1)} fusion(bf16[8192,3072]{1,0:T(8,128)(2,1)} %get-tuple-element.225, s32[]{:T(128)S(6)} %multiply.26, bf16[1,2048,3072]{2,1,0:T(8,128)(2,1)} %bitcast.78, s32[]{:T(128)S(6)} %multiply.27), kind=kOutput, calls=%fused_computation.2.clone.1 | convolution fusion | flops 12888047616 | bytes 67108872 | tf_op jit(solution)/dot_general | solution.py:14
  299.3 21.0 %collective-permute-done = bf16[128,8192]{1,0:T(8,128)(2,1)} collective-permute-done((bf16[128,8192]{1,0:T(8,128)(2,1)}, bf16[128,8192]{1,0:T(8,128)(2,1)}, u32[]{:S(2)}, u32[]{:S(2)}) %collective-permute-start) | collective-permute-done | bytes 2097184 | tf_op jit(solution)/dot_general | solution.py:14
  320.3 26.0 %collective-permute-done.1 = bf16[128,8192]{1,0:T(8,128)(2,1)} collective-permute-done((bf16[128,8192]{1,0:T(8,128)(2,1)}, bf16[128,8192]{1,0:T(8,128)(2,1)}, u32[]{:S(2)}, u32[]{:S(2)}) %collective-permute-start.1) | collective-permute-done | bytes 2097184 | tf_op jit(solution)/dot_general | solution.py:14
  346.3 6.0 fusion.72
  352.7 22.0 %fusion.73 = bf16[2,128,8192]{2,1,0:T(8,128)(2,1)} fusion(bf16[8192,3072]{1,0:T(8,128)(2,1)} %get-tuple-element.225, s32[]{:T(128)S(6)} %multiply.28, bf16[1,2048,3072]{2,1,0:T(8,128)(2,1)} %bitcast.79, s32[]{:T(128)S(6)} %multiply.29), kind=kOutput, calls=%fused_computation.clone.1 | convolution fusion | flops 12888047616 | bytes 67108872 | tf_op jit(solution)/dot_general | solution.py:14
  374.7 22.9 %collective-permute-done.2 = bf16[128,8192]{1,0:T(8,128)(2,1)} collective-permute-done((bf16[128,8192]{1,0:T(8,128)(2,1)}, bf16[128,8192]{1,0:T(8,128)(2,1)}, u32[]{:S(2)}, u32[]{:S(2)}) %collective-permute-start.2) | collective-permute-done | bytes 2097184 | tf_op jit(solution)/dot_general | solution.py:14
  397.7 5.9 fusion.74
  410.7 22.0 %fusion.71 = bf16[2,128,8192]{2,1,0:T(8,128)(2,1)} fusion(bf16[8192,3072]{1,0:T(8,128)(2,1)} %get-tuple-element.225, s32[]{:T(128)S(6)} %multiply.26, bf16[1,2048,3072]{2,1,0:T(8,128)(2,1)} %bitcast.78, s32[]{:T(128)S(6)} %multiply.27), kind=kOutput, calls=%fused_computation.2.clone.1 | convolution fusion | flops 12888047616 | bytes 67108872 | tf_op jit(solution)/dot_general | solution.py:14
  432.7 21.6 %collective-permute-done = bf16[128,8192]{1,0:T(8,128)(2,1)} collective-permute-done((bf16[128,8192]{1,0:T(8,128)(2,1)}, bf16[128,8192]{1,0:T(8,128)(2,1)}, u32[]{:S(2)}, u32[]{:S(2)}) %collective-permute-start) | collective-permute-done | bytes 2097184 | tf_op jit(solution)/dot_general | solution.py:14
  454.4 6.0 fusion.72
  462.8 22.0 %fusion.73 = bf16[2,128,8192]{2,1,0:T(8,128)(2,1)} fusion(bf16[8192,3072]{1,0:T(8,128)(2,1)} %get-tuple-element.225, s32[]{:T(128)S(6)} %multiply.28, bf16[1,2048,3072]{2,1,0:T(8,128)(2,1)} %bitcast.79, s32[]{:T(128)S(6)} %multiply.29), kind=kOutput, calls=%fused_computation.clone.1 | convolution fusion | flops 12888047616 | bytes 67108872 | tf_op jit(solution)/dot_general | solution.py:14
  484.8 21.9 %collective-permute-done.2 = bf16[128,8192]{1,0:T(8,128)(2,1)} collective-permute-done((bf16[128,8192]{1,0:T(8,128)(2,1)}, bf16[128,8192]{1,0:T(8,128)(2,1)}, u32[]{:S(2)}, u32[]{:S(2)}) %collective-permute-start.2) | collective-permute-done | bytes 2097184 | tf_op jit(solution)/dot_general | solution.py:14
  506.7 5.9 fusion.74
  519.8 22.0 %fusion.71 = bf16[2,128,8192]{2,1,0:T(8,128)(2,1)} fusion(bf16[8192,3072]{1,0:T(8,128)(2,1)} %get-tuple-element.225, s32[]{:T(128)S(6)} %multiply.26, bf16[1,2048,3072]{2,1,0:T(8,128)(2,1)} %bitcast.78, s32[]{:T(128)S(6)} %multiply.27), kind=kOutput, calls=%fused_computation.2.clone.1 | convolution fusion | flops 12888047616 | bytes 67108872 | tf_op jit(solution)/dot_general | solution.py:14
  541.8 21.9 %collective-permute-done = bf16[128,8192]{1,0:T(8,128)(2,1)} collective-permute-done((bf16[128,8192]{1,0:T(8,128)(2,1)}, bf16[128,8192]{1,0:T(8,128)(2,1)}, u32[]{:S(2)}, u32[]{:S(2)}) %collective-permute-start) | collective-permute-done | bytes 2097184 | tf_op jit(solution)/dot_general | solution.py:14
  563.7 6.0 fusion.72
  572.2 22.0 %fusion.73 = bf16[2,128,8192]{2,1,0:T(8,128)(2,1)} fusion(bf16[8192,3072]{1,0:T(8,128)(2,1)} %get-tuple-element.225, s32[]{:T(128)S(6)} %multiply.28, bf16[1,2048,3072]{2,1,0:T(8,128)(2,1)} %bitcast.79, s32[]{:T(128)S(6)} %multiply.29), kind=kOutput, calls=%fused_computation.clone.1 | convolution fusion | flops 12888047616 | bytes 67108872 | tf_op jit(solution)/dot_general | solution.py:14
  594.2 23.1 %collective-permute-done.2 = bf16[128,8192]{1,0:T(8,128)(2,1)} collective-permute-done((bf16[128,8192]{1,0:T(8,128)(2,1)}, bf16[128,8192]{1,0:T(8,128)(2,1)}, u32[]{:S(2)}, u32[]{:S(2)}) %collective-permute-start.2) | collective-permute-done | bytes 2097184 | tf_op jit(solution)/dot_general | solution.py:14
  630.4 22.0 %fusion.71 = bf16[2,128,8192]{2,1,0:T(8,128)(2,1)} fusion(bf16[8192,3072]{1,0:T(8,128)(2,1)} %get-tuple-element.225, s32[]{:T(128)S(6)} %multiply.26, bf16[1,2048,3072]{2,1,0:T(8,128)(2,1)} %bitcast.78, s32[]{:T(128)S(6)} %multiply.27), kind=kOutput, calls=%fused_computation.2.clone.1 | convolution fusion | flops 12888047616 | bytes 67108872 | tf_op jit(solution)/dot_general | solution.py:14
  652.4 21.9 %collective-permute-done = bf16[128,8192]{1,0:T(8,128)(2,1)} collective-permute-done((bf16[128,8192]{1,0:T(8,128)(2,1)}, bf16[128,8192]{1,0:T(8,128)(2,1)}, u32[]{:S(2)}, u32[]{:S(2)}) %collective-permute-start) | collective-permute-done | bytes 2097184 | tf_op jit(solution)/dot_general | solution.py:14
  674.3 6.0 fusion.72
  682.8 22.0 %fusion.73 = bf16[2,128,8192]{2,1,0:T(8,128)(2,1)} fusion(bf16[8192,3072]{1,0:T(8,128)(2,1)} %get-tuple-element.225, s32[]{:T(128)S(6)} %multiply.28, bf16[1,2048,3072]{2,1,0:T(8,128)(2,1)} %bitcast.79, s32[]{:T(128)S(6)} %multiply.29), kind=kOutput, calls=%fused_computation.clone.1 | convolution fusion | flops 12888047616 | bytes 67108872 | tf_op jit(solution)/dot_general | solution.py:14
  704.7 21.9 %collective-permute-done.2 = bf16[128,8192]{1,0:T(8,128)(2,1)} collective-permute-done((bf16[128,8192]{1,0:T(8,128)(2,1)}, bf16[128,8192]{1,0:T(8,128)(2,1)}, u32[]{:S(2)}, u32[]{:S(2)}) %collective-permute-start.2) | collective-permute-done | bytes 2097184 | tf_op jit(solution)/dot_general | solution.py:14
  735.0 457.1 %while.5 = (bf16[2048,3072]{1,0:T(8,128)(2,1)}, bf16[8192,3072]{1,0:T(8,128)(2,1)}, bf16[128,8192]{1,0:T(8,128)(2,1)S(1)}, bf16[128,8192]{1,0:T(8,128)(2,1)}, u3...) while((bf16[2048,3072]{1,0:T(8,128)(2,1)}, ...), condition=%wide.windowed_dot_general_cond_rs.1.clone, body=%wide.windowed_dot_general_body_rs.1.clone.sunk | while | flops 25782386688 | bytes 209715840 | solution.py:14
  738.6 22.0 %fusion.79 = bf16[2,128,8192]{2,1,0:T(8,128)(2,1)} fusion(bf16[8192,3072]{1,0:T(8,128)(2,1)} %get-tuple-element.189, s32[]{:T(128)S(6)} %multiply.30, bf16[1,2048,3072]{2,1,0:T(8,128)(2,1)} %bitcast.76, s32[]{:T(128)S(6)} %multiply.31), kind=kOutput, calls=%fused_computation.26.clone.1 | convolution fusion | flops 12888047616 | bytes 67108872 | tf_op jit(solution)/dot_general | solution.py:14
  760.6 42.3 %collective-permute-done.4 = bf16[128,8192]{1,0:T(8,128)(2,1)} collective-permute-done((bf16[128,8192]{1,0:T(8,128)(2,1)}, bf16[128,8192]{1,0:T(8,128)(2,1)}, u32[]{:S(2)}, u32[]{:S(2)}) %collective-permute-start.4) | collective-permute-done | bytes 2097184 | tf_op jit(solution)/dot_general | solution.py:14
  812.0 22.0 %fusion.81 = bf16[2,128,8192]{2,1,0:T(8,128)(2,1)} fusion(bf16[8192,3072]{1,0:T(8,128)(2,1)} %get-tuple-element.189, s32[]{:T(128)S(6)} %multiply.32, bf16[1,2048,3072]{2,1,0:T(8,128)(2,1)} %bitcast.77, s32[]{:T(128)S(6)} %multiply.33), kind=kOutput, calls=%fused_computation.24.clone.1 | convolution fusion | flops 12888047616 | bytes 67108872 | tf_op jit(solution)/dot_general | solution.py:14
  834.0 22.9 %collective-permute-done.6 = bf16[128,8192]{1,0:T(8,128)(2,1)S(1)} collective-permute-done((bf16[128,8192]{1,0:T(8,128)(2,1)}, bf16[128,8192]{1,0:T(8,128)(2,1)S(1)}, u32[]{:S(2)}, u32[]{:S(2)}) %collective-permute-start.6) | collective-permute-done | bytes 2097184 | tf_op jit(solution)/dot_general | solution.py:14
  870.5 22.0 %fusion.79 = bf16[2,128,8192]{2,1,0:T(8,128)(2,1)} fusion(bf16[8192,3072]{1,0:T(8,128)(2,1)} %get-tuple-element.189, s32[]{:T(128)S(6)} %multiply.30, bf16[1,2048,3072]{2,1,0:T(8,128)(2,1)} %bitcast.76, s32[]{:T(128)S(6)} %multiply.31), kind=kOutput, calls=%fused_computation.26.clone.1 | convolution fusion | flops 12888047616 | bytes 67108872 | tf_op jit(solution)/dot_general | solution.py:14
  892.5 21.5 %collective-permute-done.4 = bf16[128,8192]{1,0:T(8,128)(2,1)} collective-permute-done((bf16[128,8192]{1,0:T(8,128)(2,1)}, bf16[128,8192]{1,0:T(8,128)(2,1)}, u32[]{:S(2)}, u32[]{:S(2)}) %collective-permute-start.4) | collective-permute-done | bytes 2097184 | tf_op jit(solution)/dot_general | solution.py:14
  921.8 22.0 %fusion.81 = bf16[2,128,8192]{2,1,0:T(8,128)(2,1)} fusion(bf16[8192,3072]{1,0:T(8,128)(2,1)} %get-tuple-element.189, s32[]{:T(128)S(6)} %multiply.32, bf16[1,2048,3072]{2,1,0:T(8,128)(2,1)} %bitcast.77, s32[]{:T(128)S(6)} %multiply.33), kind=kOutput, calls=%fused_computation.24.clone.1 | convolution fusion | flops 12888047616 | bytes 67108872 | tf_op jit(solution)/dot_general | solution.py:14
  943.8 22.0 %collective-permute-done.6 = bf16[128,8192]{1,0:T(8,128)(2,1)S(1)} collective-permute-done((bf16[128,8192]{1,0:T(8,128)(2,1)}, bf16[128,8192]{1,0:T(8,128)(2,1)S(1)}, u32[]{:S(2)}, u32[]{:S(2)}) %collective-permute-start.6) | collective-permute-done | bytes 2097184 | tf_op jit(solution)/dot_general | solution.py:14
  979.4 22.0 %fusion.79 = bf16[2,128,8192]{2,1,0:T(8,128)(2,1)} fusion(bf16[8192,3072]{1,0:T(8,128)(2,1)} %get-tuple-element.189, s32[]{:T(128)S(6)} %multiply.30, bf16[1,2048,3072]{2,1,0:T(8,128)(2,1)} %bitcast.76, s32[]{:T(128)S(6)} %multiply.31), kind=kOutput, calls=%fused_computation.26.clone.1 | convolution fusion | flops 12888047616 | bytes 67108872 | tf_op jit(solution)/dot_general | solution.py:14
  1001.3 22.0 %collective-permute-done.4 = bf16[128,8192]{1,0:T(8,128)(2,1)} collective-permute-done((bf16[128,8192]{1,0:T(8,128)(2,1)}, bf16[128,8192]{1,0:T(8,128)(2,1)}, u32[]{:S(2)}, u32[]{:S(2)}) %collective-permute-start.4) | collective-permute-done | bytes 2097184 | tf_op jit(solution)/dot_general | solution.py:14
  1031.1 22.0 %fusion.81 = bf16[2,128,8192]{2,1,0:T(8,128)(2,1)} fusion(bf16[8192,3072]{1,0:T(8,128)(2,1)} %get-tuple-element.189, s32[]{:T(128)S(6)} %multiply.32, bf16[1,2048,3072]{2,1,0:T(8,128)(2,1)} %bitcast.77, s32[]{:T(128)S(6)} %multiply.33), kind=kOutput, calls=%fused_computation.24.clone.1 | convolution fusion | flops 12888047616 | bytes 67108872 | tf_op jit(solution)/dot_general | solution.py:14
  1053.1 22.7 %collective-permute-done.6 = bf16[128,8192]{1,0:T(8,128)(2,1)S(1)} collective-permute-done((bf16[128,8192]{1,0:T(8,128)(2,1)}, bf16[128,8192]{1,0:T(8,128)(2,1)S(1)}, u32[]{:S(2)}, u32[]{:S(2)}) %collective-permute-start.6) | collective-permute-done | bytes 2097184 | tf_op jit(solution)/dot_general | solution.py:14
  1089.4 22.0 %fusion.79 = bf16[2,128,8192]{2,1,0:T(8,128)(2,1)} fusion(bf16[8192,3072]{1,0:T(8,128)(2,1)} %get-tuple-element.189, s32[]{:T(128)S(6)} %multiply.30, bf16[1,2048,3072]{2,1,0:T(8,128)(2,1)} %bitcast.76, s32[]{:T(128)S(6)} %multiply.31), kind=kOutput, calls=%fused_computation.26.clone.1 | convolution fusion | flops 12888047616 | bytes 67108872 | tf_op jit(solution)/dot_general | solution.py:14
  1111.4 22.0 %collective-permute-done.4 = bf16[128,8192]{1,0:T(8,128)(2,1)} collective-permute-done((bf16[128,8192]{1,0:T(8,128)(2,1)}, bf16[128,8192]{1,0:T(8,128)(2,1)}, u32[]{:S(2)}, u32[]{:S(2)}) %collective-permute-start.4) | collective-permute-done | bytes 2097184 | tf_op jit(solution)/dot_general | solution.py:14
  1141.1 22.0 %fusion.81 = bf16[2,128,8192]{2,1,0:T(8,128)(2,1)} fusion(bf16[8192,3072]{1,0:T(8,128)(2,1)} %get-tuple-element.189, s32[]{:T(128)S(6)} %multiply.32, bf16[1,2048,3072]{2,1,0:T(8,128)(2,1)} %bitcast.77, s32[]{:T(128)S(6)} %multiply.33), kind=kOutput, calls=%fused_computation.24.clone.1 | convolution fusion | flops 12888047616 | bytes 67108872 | tf_op jit(solution)/dot_general | solution.py:14
  1163.1 22.4 %collective-permute-done.6 = bf16[128,8192]{1,0:T(8,128)(2,1)S(1)} collective-permute-done((bf16[128,8192]{1,0:T(8,128)(2,1)}, bf16[128,8192]{1,0:T(8,128)(2,1)S(1)}, u32[]{:S(2)}, u32[]{:S(2)}) %collective-permute-start.6) | collective-permute-done | bytes 2097184 | tf_op jit(solution)/dot_general | solution.py:14
  1194.6 126.7 %convolution_convert_fusion = bf16[3072,8192]{1,0:T(8,128)(2,1)} fusion(bf16[2048,8192]{1,0:T(8,128)(2,1)} %all-gather.7.cloned.1.call-done, bf16[2048,3072]{1,0:T(8,128)(2,1)} %param.6, bf16[2048,3072]{1,0:T(8,128)(2,1)} %param.7), kind=kOutput, calls=%fused_computation.50 | convolution fusion | flops 103154712576 | bytes 109051904 | tf_op jit(solution)/gta,gtb->gab/dot_general | solution.py:19
  1321.3 114.9 %convert_bitcast_fusion.1 = bf16[8192,3072]{0,1:T(8,128)(2,1)} fusion(bf16[2048,3072]{1,0:T(8,128)(2,1)} %get-tuple-element.249, bf16[2048,8192]{1,0:T(8,128)(2,1)} %all-gather.9.cloned.1.call-done), kind=kOutput, calls=%fused_computation.49 | convolution fusion | flops 103104380928 | bytes 96468992 | tf_op jit(solution)/gta,gtb->gab/dot_general | solution.py:19
  1436.2 114.5 %convert_bitcast_fusion = bf16[8192,3072]{0,1:T(8,128)(2,1)} fusion(bf16[2048,3072]{1,0:T(8,128)(2,1)} %get-tuple-element.248, bf16[2048,8192]{1,0:T(8,128)(2,1)} %all-gather.9.cloned.1.call-done), kind=kOutput, calls=%fused_computation.48 | convolution fusion | flops 103104380928 | bytes 96468992 | tf_op jit(solution)/gta,gtb->gab/dot_general | solution.py:19
  1550.6 64.5 %copy = bf16[8192,3072]{1,0:T(8,128)(2,1)} copy(bf16[8192,3072]{0,1:T(8,128)(2,1)} %convert_bitcast_fusion.1) | data formatting | bytes 100663296
  1615.1 64.6 %copy.1 = bf16[8192,3072]{1,0:T(8,128)(2,1)} copy(bf16[8192,3072]{0,1:T(8,128)(2,1)} %convert_bitcast_fusion) | data formatting | bytes 100663296
  (109 shorter events, 140.0 us)
Async XLA Ops:
  7.2 136.7 %all-gather.7.cloned.1.call-start = ((), (), s32[]{:S(2)}) async-start(), calls=%async_computation | async-start | bytes 35651584 | tf_op args[1]
  7.9 1313.4 %all-gather.9.cloned.1.call-start = ((), (), s32[]{:S(2)}) async-start(), calls=%async_computation.1 | async-start | bytes 35651584 | tf_op args[0]
  272.6 462.5 %copy-start = (bf16[128,8192]{1,0:T(8,128)(2,1)S(1)}, bf16[128,8192]{1,0:T(8,128)(2,1)}, u32[]{:S(2)}) copy-start(bf16[128,8192]{1,0:T(8,128)(2,1)} %custom-call.2) | copy-start | bytes 6291460
  273.0 2.5 copy-start.3
  274.5 45.8 %collective-permute-start = (bf16[128,8192]{1,0:T(8,128)(2,1)}, bf16[128,8192]{1,0:T(8,128)(2,1)}, u32[]{:S(2)}, u32[]{:S(2)}) collective-permute-start(bf16[128,8192]{1,0:T(8,128)(2,1)} %broadcast_select_fusion.8), channel_id=4, source_target_pairs={{0,1},{1,2},{2,3},{3,4},{4,5},{5,6},{6,7},{7,8},{8,9},{9,10},{10,1... | collective-permute-start | bytes 6291464 | tf_op jit(solution)/dot_general | solution.py:14
  277.1 69.2 %collective-permute-start.1 = (bf16[128,8192]{1,0:T(8,128)(2,1)}, bf16[128,8192]{1,0:T(8,128)(2,1)}, u32[]{:S(2)}, u32[]{:S(2)}) collective-permute-start(bf16[128,8192]{1,0:T(8,128)(2,1)} %broadcast_select_fusion.9), channel_id=3, source_target_pairs={{0,15},{1,0},{2,1},{3,2},{4,3},{5,4},{6,5},{7,6},{8,7},{9,8},{10,9... | collective-permute-start | bytes 6291464 | tf_op jit(solution)/dot_general | solution.py:14
  352.2 45.4 %collective-permute-start.2 = (bf16[128,8192]{1,0:T(8,128)(2,1)}, bf16[128,8192]{1,0:T(8,128)(2,1)}, u32[]{:S(2)}, u32[]{:S(2)}) collective-permute-start(bf16[128,8192]{1,0:T(8,128)(2,1)} %get-tuple-element.151), channel_id=6, source_target_pairs={{0,1},{1,2},{2,3},{3,4},{4,5},{5,6},{6,7},{7,8},{8,9},{9,10},{10,1... | collective-permute-start | bytes 6291464 | tf_op jit(solution)/dot_general | solution.py:14
  352.2 45.4 %collective-permute-start.3 = (bf16[128,8192]{1,0:T(8,128)(2,1)}, bf16[128,8192]{1,0:T(8,128)(2,1)}, u32[]{:S(2)}, u32[]{:S(2)}) collective-permute-start(bf16[128,8192]{1,0:T(8,128)(2,1)} %get-tuple-element.152), channel_id=5, source_target_pairs={{0,15},{1,0},{2,1},{3,2},{4,3},{5,4},{6,5},{7,6},{8,7},{9,8},{10,9... | collective-permute-start | bytes 6291464 | tf_op jit(solution)/dot_general | solution.py:14
  403.5 5.7 copy-start.3
  406.7 47.6 %collective-permute-start = (bf16[128,8192]{1,0:T(8,128)(2,1)}, bf16[128,8192]{1,0:T(8,128)(2,1)}, u32[]{:S(2)}, u32[]{:S(2)}) collective-permute-start(bf16[128,8192]{1,0:T(8,128)(2,1)} %broadcast_select_fusion.8), channel_id=4, source_target_pairs={{0,1},{1,2},{2,3},{3,4},{4,5},{5,6},{6,7},{7,8},{8,9},{9,10},{10,1... | collective-permute-start | bytes 6291464 | tf_op jit(solution)/dot_general | solution.py:14
  410.7 43.6 %collective-permute-start.1 = (bf16[128,8192]{1,0:T(8,128)(2,1)}, bf16[128,8192]{1,0:T(8,128)(2,1)}, u32[]{:S(2)}, u32[]{:S(2)}) collective-permute-start(bf16[128,8192]{1,0:T(8,128)(2,1)} %broadcast_select_fusion.9), channel_id=3, source_target_pairs={{0,15},{1,0},{2,1},{3,2},{4,3},{5,4},{6,5},{7,6},{8,7},{9,8},{10,9... | collective-permute-start | bytes 6291464 | tf_op jit(solution)/dot_general | solution.py:14
  460.3 46.4 %collective-permute-start.2 = (bf16[128,8192]{1,0:T(8,128)(2,1)}, bf16[128,8192]{1,0:T(8,128)(2,1)}, u32[]{:S(2)}, u32[]{:S(2)}) collective-permute-start(bf16[128,8192]{1,0:T(8,128)(2,1)} %get-tuple-element.151), channel_id=6, source_target_pairs={{0,1},{1,2},{2,3},{3,4},{4,5},{5,6},{6,7},{7,8},{8,9},{9,10},{10,1... | collective-permute-start | bytes 6291464 | tf_op jit(solution)/dot_general | solution.py:14
  462.8 43.9 %collective-permute-start.3 = (bf16[128,8192]{1,0:T(8,128)(2,1)}, bf16[128,8192]{1,0:T(8,128)(2,1)}, u32[]{:S(2)}, u32[]{:S(2)}) collective-permute-start(bf16[128,8192]{1,0:T(8,128)(2,1)} %get-tuple-element.152), channel_id=5, source_target_pairs={{0,15},{1,0},{2,1},{3,2},{4,3},{5,4},{6,5},{7,6},{8,7},{9,8},{10,9... | collective-permute-start | bytes 6291464 | tf_op jit(solution)/dot_general | solution.py:14
  512.6 5.7 copy-start.3
  515.8 47.9 %collective-permute-start = (bf16[128,8192]{1,0:T(8,128)(2,1)}, bf16[128,8192]{1,0:T(8,128)(2,1)}, u32[]{:S(2)}, u32[]{:S(2)}) collective-permute-start(bf16[128,8192]{1,0:T(8,128)(2,1)} %broadcast_select_fusion.8), channel_id=4, source_target_pairs={{0,1},{1,2},{2,3},{3,4},{4,5},{5,6},{6,7},{7,8},{8,9},{9,10},{10,1... | collective-permute-start | bytes 6291464 | tf_op jit(solution)/dot_general | solution.py:14
  519.8 43.9 %collective-permute-start.1 = (bf16[128,8192]{1,0:T(8,128)(2,1)}, bf16[128,8192]{1,0:T(8,128)(2,1)}, u32[]{:S(2)}, u32[]{:S(2)}) collective-permute-start(bf16[128,8192]{1,0:T(8,128)(2,1)} %broadcast_select_fusion.9), channel_id=3, source_target_pairs={{0,15},{1,0},{2,1},{3,2},{4,3},{5,4},{6,5},{7,6},{8,7},{9,8},{10,9... | collective-permute-start | bytes 6291464 | tf_op jit(solution)/dot_general | solution.py:14
  569.7 47.6 %collective-permute-start.2 = (bf16[128,8192]{1,0:T(8,128)(2,1)}, bf16[128,8192]{1,0:T(8,128)(2,1)}, u32[]{:S(2)}, u32[]{:S(2)}) collective-permute-start(bf16[128,8192]{1,0:T(8,128)(2,1)} %get-tuple-element.151), channel_id=6, source_target_pairs={{0,1},{1,2},{2,3},{3,4},{4,5},{5,6},{6,7},{7,8},{8,9},{9,10},{10,1... | collective-permute-start | bytes 6291464 | tf_op jit(solution)/dot_general | solution.py:14
  572.2 45.1 %collective-permute-start.3 = (bf16[128,8192]{1,0:T(8,128)(2,1)}, bf16[128,8192]{1,0:T(8,128)(2,1)}, u32[]{:S(2)}, u32[]{:S(2)}) collective-permute-start(bf16[128,8192]{1,0:T(8,128)(2,1)} %get-tuple-element.152), channel_id=5, source_target_pairs={{0,15},{1,0},{2,1},{3,2},{4,3},{5,4},{6,5},{7,6},{8,7},{9,8},{10,9... | collective-permute-start | bytes 6291464 | tf_op jit(solution)/dot_general | solution.py:14
  623.2 5.7 copy-start.3
  626.4 47.9 %collective-permute-start = (bf16[128,8192]{1,0:T(8,128)(2,1)}, bf16[128,8192]{1,0:T(8,128)(2,1)}, u32[]{:S(2)}, u32[]{:S(2)}) collective-permute-start(bf16[128,8192]{1,0:T(8,128)(2,1)} %broadcast_select_fusion.8), channel_id=4, source_target_pairs={{0,1},{1,2},{2,3},{3,4},{4,5},{5,6},{6,7},{7,8},{8,9},{9,10},{10,1... | collective-permute-start | bytes 6291464 | tf_op jit(solution)/dot_general | solution.py:14
  630.4 43.9 %collective-permute-start.1 = (bf16[128,8192]{1,0:T(8,128)(2,1)}, bf16[128,8192]{1,0:T(8,128)(2,1)}, u32[]{:S(2)}, u32[]{:S(2)}) collective-permute-start(bf16[128,8192]{1,0:T(8,128)(2,1)} %broadcast_select_fusion.9), channel_id=3, source_target_pairs={{0,15},{1,0},{2,1},{3,2},{4,3},{5,4},{6,5},{7,6},{8,7},{9,8},{10,9... | collective-permute-start | bytes 6291464 | tf_op jit(solution)/dot_general | solution.py:14
  680.3 46.4 %collective-permute-start.2 = (bf16[128,8192]{1,0:T(8,128)(2,1)}, bf16[128,8192]{1,0:T(8,128)(2,1)}, u32[]{:S(2)}, u32[]{:S(2)}) collective-permute-start(bf16[128,8192]{1,0:T(8,128)(2,1)} %get-tuple-element.151), channel_id=6, source_target_pairs={{0,1},{1,2},{2,3},{3,4},{4,5},{5,6},{6,7},{7,8},{8,9},{9,10},{10,1... | collective-permute-start | bytes 6291464 | tf_op jit(solution)/dot_general | solution.py:14
  682.8 43.9 %collective-permute-start.3 = (bf16[128,8192]{1,0:T(8,128)(2,1)}, bf16[128,8192]{1,0:T(8,128)(2,1)}, u32[]{:S(2)}, u32[]{:S(2)}) collective-permute-start(bf16[128,8192]{1,0:T(8,128)(2,1)} %get-tuple-element.152), channel_id=5, source_target_pairs={{0,15},{1,0},{2,1},{3,2},{4,3},{5,4},{6,5},{7,6},{8,7},{9,8},{10,9... | collective-permute-start | bytes 6291464 | tf_op jit(solution)/dot_general | solution.py:14
  732.5 947.2 %collective-permute-start.8 = (bf16[128,8192]{1,0:T(8,128)(2,1)}, bf16[128,8192]{1,0:T(8,128)(2,1)}, u32[]{:S(2)}, u32[]{:S(2)}) collective-permute-start(bf16[128,8192]{1,0:T(8,128)(2,1)} %get-tuple-element.13), channel_id=7, source_target_pairs={{0,1},{1,2},{2,3},{3,4},{4,5},{5,6},{6,7},{7,8},{8,9},{9,10},{10,1... | collective-permute-start | bytes 6291464 | tf_op jit(solution)/dot_general | solution.py:14
  736.7 66.3 %collective-permute-start.4 = (bf16[128,8192]{1,0:T(8,128)(2,1)}, bf16[128,8192]{1,0:T(8,128)(2,1)}, u32[]{:S(2)}, u32[]{:S(2)}) collective-permute-start(bf16[128,8192]{1,0:T(8,128)(2,1)} %broadcast_select_fusion.10), channel_id=10, source_target_pairs={{0,1},{1,2},{2,3},{3,4},{4,5},{5,6},{6,7},{7,8},{8,9},{9,10},{10,1... | collective-permute-start | bytes 6291464 | tf_op jit(solution)/dot_general | solution.py:14
  738.2 68.0 %collective-permute-start.5 = (bf16[128,8192]{1,0:T(8,128)(2,1)}, bf16[128,8192]{1,0:T(8,128)(2,1)S(1)}, u32[]{:S(2)}, u32[]{:S(2)}) collective-permute-start(bf16[128,8192]{1,0:T(8,128)(2,1)} %broadcast_select_fusion.11), channel_id=9, source_target_pairs={{0,15},{1,0},{2,1},{3,2},{4,3},{5,4},{6,5},{7,6},{8,7},{9,8},{10,9... | collective-permute-start | bytes 6291464 | tf_op jit(solution)/dot_general | solution.py:14
  811.5 45.4 %collective-permute-start.6 = (bf16[128,8192]{1,0:T(8,128)(2,1)}, bf16[128,8192]{1,0:T(8,128)(2,1)S(1)}, u32[]{:S(2)}, u32[]{:S(2)}) collective-permute-start(bf16[128,8192]{1,0:T(8,128)(2,1)} %get-tuple-element.160), channel_id=12, source_target_pairs={{0,1},{1,2},{2,3},{3,4},{4,5},{5,6},{6,7},{7,8},{8,9},{9,10},{10,1... | collective-permute-start | bytes 6291464 | tf_op jit(solution)/dot_general | solution.py:14
  811.5 46.7 %collective-permute-start.7 = (bf16[128,8192]{1,0:T(8,128)(2,1)}, bf16[128,8192]{1,0:T(8,128)(2,1)}, u32[]{:S(2)}, u32[]{:S(2)}) collective-permute-start(bf16[128,8192]{1,0:T(8,128)(2,1)} %get-tuple-element.161), channel_id=11, source_target_pairs={{0,15},{1,0},{2,1},{3,2},{4,3},{5,4},{6,5},{7,6},{8,7},{9,8},{10,9... | collective-permute-start | bytes 6291464 | tf_op jit(solution)/dot_general | solution.py:14
  856.9 1.3 copy-start.4
  866.5 47.5 %collective-permute-start.4 = (bf16[128,8192]{1,0:T(8,128)(2,1)}, bf16[128,8192]{1,0:T(8,128)(2,1)}, u32[]{:S(2)}, u32[]{:S(2)}) collective-permute-start(bf16[128,8192]{1,0:T(8,128)(2,1)} %broadcast_select_fusion.10), channel_id=10, source_target_pairs={{0,1},{1,2},{2,3},{3,4},{4,5},{5,6},{6,7},{7,8},{8,9},{9,10},{10,1... | collective-permute-start | bytes 6291464 | tf_op jit(solution)/dot_general | solution.py:14
  870.5 43.5 %collective-permute-start.5 = (bf16[128,8192]{1,0:T(8,128)(2,1)}, bf16[128,8192]{1,0:T(8,128)(2,1)S(1)}, u32[]{:S(2)}, u32[]{:S(2)}) collective-permute-start(bf16[128,8192]{1,0:T(8,128)(2,1)} %broadcast_select_fusion.11), channel_id=9, source_target_pairs={{0,15},{1,0},{2,1},{3,2},{4,3},{5,4},{6,5},{7,6},{8,7},{9,8},{10,9... | collective-permute-start | bytes 6291464 | tf_op jit(solution)/dot_general | solution.py:14
  919.3 46.5 %collective-permute-start.6 = (bf16[128,8192]{1,0:T(8,128)(2,1)}, bf16[128,8192]{1,0:T(8,128)(2,1)S(1)}, u32[]{:S(2)}, u32[]{:S(2)}) collective-permute-start(bf16[128,8192]{1,0:T(8,128)(2,1)} %get-tuple-element.160), channel_id=12, source_target_pairs={{0,1},{1,2},{2,3},{3,4},{4,5},{5,6},{6,7},{7,8},{8,9},{9,10},{10,1... | collective-permute-start | bytes 6291464 | tf_op jit(solution)/dot_general | solution.py:14
  921.8 45.3 %collective-permute-start.7 = (bf16[128,8192]{1,0:T(8,128)(2,1)}, bf16[128,8192]{1,0:T(8,128)(2,1)}, u32[]{:S(2)}, u32[]{:S(2)}) collective-permute-start(bf16[128,8192]{1,0:T(8,128)(2,1)} %get-tuple-element.161), channel_id=11, source_target_pairs={{0,15},{1,0},{2,1},{3,2},{4,3},{5,4},{6,5},{7,6},{8,7},{9,8},{10,9... | collective-permute-start | bytes 6291464 | tf_op jit(solution)/dot_general | solution.py:14
  965.8 1.3 copy-start.4
  975.4 47.9 %collective-permute-start.4 = (bf16[128,8192]{1,0:T(8,128)(2,1)}, bf16[128,8192]{1,0:T(8,128)(2,1)}, u32[]{:S(2)}, u32[]{:S(2)}) collective-permute-start(bf16[128,8192]{1,0:T(8,128)(2,1)} %broadcast_select_fusion.10), channel_id=10, source_target_pairs={{0,1},{1,2},{2,3},{3,4},{4,5},{5,6},{6,7},{7,8},{8,9},{9,10},{10,1... | collective-permute-start | bytes 6291464 | tf_op jit(solution)/dot_general | solution.py:14
  979.4 44.0 %collective-permute-start.5 = (bf16[128,8192]{1,0:T(8,128)(2,1)}, bf16[128,8192]{1,0:T(8,128)(2,1)S(1)}, u32[]{:S(2)}, u32[]{:S(2)}) collective-permute-start(bf16[128,8192]{1,0:T(8,128)(2,1)} %broadcast_select_fusion.11), channel_id=9, source_target_pairs={{0,15},{1,0},{2,1},{3,2},{4,3},{5,4},{6,5},{7,6},{8,7},{9,8},{10,9... | collective-permute-start | bytes 6291464 | tf_op jit(solution)/dot_general | solution.py:14
  1028.6 47.2 %collective-permute-start.6 = (bf16[128,8192]{1,0:T(8,128)(2,1)}, bf16[128,8192]{1,0:T(8,128)(2,1)S(1)}, u32[]{:S(2)}, u32[]{:S(2)}) collective-permute-start(bf16[128,8192]{1,0:T(8,128)(2,1)} %get-tuple-element.160), channel_id=12, source_target_pairs={{0,1},{1,2},{2,3},{3,4},{4,5},{5,6},{6,7},{7,8},{8,9},{9,10},{10,1... | collective-permute-start | bytes 6291464 | tf_op jit(solution)/dot_general | solution.py:14
  1031.1 46.0 %collective-permute-start.7 = (bf16[128,8192]{1,0:T(8,128)(2,1)}, bf16[128,8192]{1,0:T(8,128)(2,1)}, u32[]{:S(2)}, u32[]{:S(2)}) collective-permute-start(bf16[128,8192]{1,0:T(8,128)(2,1)} %get-tuple-element.161), channel_id=11, source_target_pairs={{0,15},{1,0},{2,1},{3,2},{4,3},{5,4},{6,5},{7,6},{8,7},{9,8},{10,9... | collective-permute-start | bytes 6291464 | tf_op jit(solution)/dot_general | solution.py:14
  1075.8 1.3 copy-start.4
  1085.4 47.9 %collective-permute-start.4 = (bf16[128,8192]{1,0:T(8,128)(2,1)}, bf16[128,8192]{1,0:T(8,128)(2,1)}, u32[]{:S(2)}, u32[]{:S(2)}) collective-permute-start(bf16[128,8192]{1,0:T(8,128)(2,1)} %broadcast_select_fusion.10), channel_id=10, source_target_pairs={{0,1},{1,2},{2,3},{3,4},{4,5},{5,6},{6,7},{7,8},{8,9},{9,10},{10,1... | collective-permute-start | bytes 6291464 | tf_op jit(solution)/dot_general | solution.py:14
  1089.4 44.0 %collective-permute-start.5 = (bf16[128,8192]{1,0:T(8,128)(2,1)}, bf16[128,8192]{1,0:T(8,128)(2,1)S(1)}, u32[]{:S(2)}, u32[]{:S(2)}) collective-permute-start(bf16[128,8192]{1,0:T(8,128)(2,1)} %broadcast_select_fusion.11), channel_id=9, source_target_pairs={{0,15},{1,0},{2,1},{3,2},{4,3},{5,4},{6,5},{7,6},{8,7},{9,8},{10,9... | collective-permute-start | bytes 6291464 | tf_op jit(solution)/dot_general | solution.py:14
  1138.6 46.9 %collective-permute-start.6 = (bf16[128,8192]{1,0:T(8,128)(2,1)}, bf16[128,8192]{1,0:T(8,128)(2,1)S(1)}, u32[]{:S(2)}, u32[]{:S(2)}) collective-permute-start(bf16[128,8192]{1,0:T(8,128)(2,1)} %get-tuple-element.160), channel_id=12, source_target_pairs={{0,1},{1,2},{2,3},{3,4},{4,5},{5,6},{6,7},{7,8},{8,9},{9,10},{10,1... | collective-permute-start | bytes 6291464 | tf_op jit(solution)/dot_general | solution.py:14
  1141.1 45.7 %collective-permute-start.7 = (bf16[128,8192]{1,0:T(8,128)(2,1)}, bf16[128,8192]{1,0:T(8,128)(2,1)}, u32[]{:S(2)}, u32[]{:S(2)}) collective-permute-start(bf16[128,8192]{1,0:T(8,128)(2,1)} %get-tuple-element.161), channel_id=11, source_target_pairs={{0,15},{1,0},{2,1},{3,2},{4,3},{5,4},{6,5},{7,6},{8,7},{9,8},{10,9... | collective-permute-start | bytes 6291464 | tf_op jit(solution)/dot_general | solution.py:14
  1185.5 1.3 copy-start.4
  1192.1 129.2 %copy-start.1 = (bf16[128,8192]{1,0:T(8,128)(2,1)}, bf16[128,8192]{1,0:T(8,128)(2,1)S(1)}, u32[]{:S(2)}) copy-start(bf16[128,8192]{1,0:T(8,128)(2,1)S(1)} %get-tuple-element.14) | copy-start | bytes 6291460
  1192.1 487.6 %collective-permute-start.9 = (bf16[128,8192]{1,0:T(8,128)(2,1)}, bf16[128,8192]{1,0:T(8,128)(2,1)}, u32[]{:S(2)}, u32[]{:S(2)}) collective-permute-start(bf16[128,8192]{1,0:T(8,128)(2,1)} %get-tuple-element.15), channel_id=13, source_target_pairs={{0,1},{1,2},{2,3},{3,4},{4,5},{5,6},{6,7},{7,8},{8,9},{9,10},{10,1... | collective-permute-start | bytes 6291464 | tf_op jit(solution)/dot_general | solution.py:14
  1615.1 64.6 %copy-start.2 = (bf16[128,8192]{1,0:T(8,128)(2,1)S(1)}, bf16[128,8192]{1,0:T(8,128)(2,1)}, u32[]{:S(2)}) copy-start(bf16[128,8192]{1,0:T(8,128)(2,1)} %copy-done.1) | copy-start | bytes 6291460
Sparse Core Ops, SparseCore 0:
  10.2 133.5 all-gather.6
  146.1 132.8 all-gather.8
where the time goes:
time: 1700 us; the launch traced here: 1690 us
  matrix products  836 us (49%)
  waiting for transfers between devices  540 us (32%)
  local copies, waits for them, and re-layouts  135 us (8%)
  other arithmetic  128 us (8%)
  starting transfers between devices  37.3 us (2%)
    dot_general x34, waiting for transfers between devices, step(): dx = jnp.dot(d_gate, w_gate.T) + jnp.dot(d_up, w_up.T)  404 us
    dot_general x3, matrix products, by_group(): jnp.einsum('gta,gtb->gab', a, b, preferred_element_type=jnp.float32)  356 us
    dot_general x16, matrix products, step(): dx = jnp.dot(d_gate, w_gate.T) + jnp.dot(d_up, w_up.T)  352 us
    unnamed x4, waiting for transfers between devices  137 us
    unnamed x8, local copies, waits for them, and re-layouts  129 us
    dot_general x1, matrix products, step(): d_hidden = jnp.dot(dy, w_down.T, preferred_element_type=jnp.float32)  129 us
    dot_general x16, other arithmetic, step(): dx = jnp.dot(d_gate, w_gate.T) + jnp.dot(d_up, w_up.T)  89.5 us
    dot_general x34, starting transfers between devices, step(): dx = jnp.dot(d_gate, w_gate.T) + jnp.dot(d_up, w_up.T)  37.2 us
  transfers between devices with their start and end apart: 36, of which 19 were waited for; matrix products, arithmetic and copies ran while one was open for 64% of the time, Pallas kernels for 0%

commit v1 on v0

v1 whole, which is shorter than its diff:
```python
import jax
import jax.numpy as jnp
from jax import lax
from jax.sharding import PartitionSpec as P


def act(gate, up):
    return jax.nn.silu(gate) * up


def solution(mesh):
    rows = P(("dp", "tp"), None)
    cols = P("dp", "tp")
    wcol = P(None, "tp")
    wrow = P("tp", None)

    def body(x, dy, gate, up, w_gate, w_up, w_down):
        f32, bf16 = jnp.float32, jnp.bfloat16
        dy = lax.all_gather(dy, "tp", axis=0, tiled=True)
        x = lax.all_gather(x, "tp", axis=0, tiled=True)
        hidden, back = jax.vjp(act, gate.astype(f32), up.astype(f32))
        d_hidden = lax.dot_general(dy, w_down, (((1,), (1,)), ((), ())), preferred_element_type=f32)
        d_gate, d_up = (g.astype(bf16) for g in back(d_hidden))
        nt = (((1,), (1,)), ((), ()))
        tn = (((0,), (0,)), ((), ()))
        dx = lax.dot_general(d_gate, w_gate, nt, preferred_element_type=f32)
        dx = dx + lax.dot_general(d_up, w_up, nt, preferred_element_type=f32)
        dx = lax.psum_scatter(dx.astype(bf16), "tp", scatter_dimension=0, tiled=True)
        dwd = lax.dot_general(hidden.astype(bf16), dy, tn, preferred_element_type=f32).astype(bf16)
        dwg = lax.dot_general(x, d_gate, tn, preferred_element_type=f32).astype(bf16)
        dwu = lax.dot_general(x, d_up, tn, preferred_element_type=f32).astype(bf16)
        return dx, dwg, dwu, dwd

    return jax.shard_map(
        body,
        mesh=mesh,
        in_specs=(rows, rows, cols, cols, wcol, wcol, wrow),
        out_specs=(rows, cols, cols, P(("dp", "tp"), None)),
        check_vma=False,
    )
```

time: 1700 us -> 1050 us (0.62)
  waiting for transfers between devices: 540 us -> 137 us
  other arithmetic: 128 us -> 19.1 us
  matrix products: 836 us -> 740 us
  starting transfers between devices: 37.3 us -> 0.11 us
    dot_general x34 -> x0, waiting for transfers between devices: 404 us -> none  [step(): dx = jnp.dot(d_gate, w_gate.T) + jnp.dot(d_up, w_up.T)]
    all_gather x0 -> x2, waiting for transfers between devices: none -> 135 us  [the longest x1 135 us: body(): dy = lax.all_gather(dy, 'tp', axis=0, tiled=True)]
    unnamed x4 -> x3, waiting for transfers between devices: 137 us -> 1.39 us
    dot_general x32 -> x1, other arithmetic: 123 us -> 19.1 us  [body(): dx = dx + lax.dot_general(d_up, w_up, nt, preferred_element_type=f32)]
    dot_general x20 -> x6, matrix products: 836 us -> 740 us  [the longest x1 129 us: body(): dx = lax.dot_general(d_gate, w_gate, nt, preferred_element_type=f32)]
    dot_general x34 -> x0, starting transfers between devices: 37.2 us -> none  [step(): dx = jnp.dot(d_gate, w_gate.T) + jnp.dot(d_up, w_up.T)]
    unnamed x8 -> x2, local copies, waits for them, and re-layouts: 129 us -> 129 us
  transfers between devices with their start and end apart: 36 -> 3, of which waited for: 19 -> 1; matrix products, arithmetic and copies ran while one was open for 64% -> 85% of each run, Pallas kernels for 0% -> 0%
where the time goes in v1:
time: 1050 us; the launch traced here: 1040 us
  matrix products  740 us (70%)
  waiting for transfers between devices  137 us (13%)
  local copies, waits for them, and re-layouts  129 us (12%)
  other arithmetic  19.1 us (2%)
  between operations  14.2 us (1%)
    all_gather x1, waiting for transfers between devices, body(): dy = lax.all_gather(dy, 'tp', axis=0, tiled=True)  135 us
    dot_general x1, matrix products, body(): dx = lax.dot_general(d_gate, w_gate, nt, preferred_element_type=f32)  129 us
    unnamed x2, local copies, waits for them, and re-layouts  129 us
    dot_general x1, matrix products, body(): lax.dot_general(dy, w_down, (((1,), (1,)), ((), ())), preferred_element_t...  128 us
    dot_general x1, matrix products, body(): lax.dot_general(hidden.astype(bf16), dy, tn, preferred_element_type=f32)  127 us
    dot_general x1, matrix products, body(): dwu = lax.dot_general(x, d_up, tn, preferred_element_type=f32).astype(bf16)  125 us
    dot_general x1, matrix products, body(): dx = dx + lax.dot_general(d_up, w_up, nt, preferred_element_type=f32)  116 us
    dot_general x1, matrix products, body(): lax.dot_general(x, d_gate, tn, preferred_element_type=f32).astype(bf16)  115 us
  transfers between devices with their start and end apart: 3, of which 1 were waited for; matrix products, arithmetic and copies ran while one was open for 85% of the time, Pallas kernels for 0%

profile of v1, /device:TPU:1, one launch (start us, length us, event | category | flops | bytes accessed | tf_op | source)
XLA Modules:
  0.0 1038.7 jit_solution(15159498150400500085)
XLA Ops:
  7.2 0.0 all-gather.3.cloned.1.call-start
  7.2 0.7 all-gather.3.cloned.1.call-update
  7.9 0.0 all-gather.5.cloned.1.call-start
  7.9 0.7 all-gather.5.cloned.1.call-update
  8.6 0.0 reduce-scatter.2.cloned.1.call-start
  8.7 135.2 %all-gather.3.cloned.1.call-done = bf16[2048,8192]{1,0:T(8,128)(2,1)} async-done(((bf16[128,8192]{1,0:T(8,128)(2,1)}), bf16[2048,8192]{1,0:T(8,128)(2,1)}) %all-gather.3.cloned.1.call-update) | async-done | bytes 33554448 | tf_op jit(solution)/shard_map/all_gather | solution.py:19
  143.9 128.2 %fusion.6 = (bf16[2048,3072]{1,0:T(8,128)(2,1)}, f32[2048,3072]{1,0:T(8,128)}) fusion(bf16[2048,3072]{1,0:T(8,128)(2,1)} %param.9, bf16[2048,3072]{1,0:T(8,128)(2,1)} %param.10, bf16[2048,8192]{1,0:T(8,128)(2,1)} %all-gather.3.cloned.1.call-done, bf16[3072,8192]{1,0:T(8,128)(2,1)} %param.13), kind=kOutput, calls=%fused_computation.16 | convolution fusion | flops 103161004032 | bytes 146800640 | tf_op jit(solution)/shard_map/dot_general | solution.py:22
  272.0 19.1 %multiply_convert_fusion.7 = bf16[2048,3072]{1,0:T(8,128)(2,1)} fusion(f32[2048,3072]{1,0:T(8,128)} %get-tuple-element.9, bf16[2048,3072]{1,0:T(8,128)(2,1)} %param.9), kind=kLoop, calls=%fused_computation.17.clone.1.clone.1 | loop fusion | flops 44040192 | bytes 50331648 | tf_op jit(solution)/shard_map/dot_general | solution.py:27
  291.1 129.3 %fusion.9 = f32[2048,8192]{1,0:T(8,128)} fusion(bf16[2048,3072]{1,0:T(8,128)(2,1)} %get-tuple-element.8, bf16[8192,3072]{1,0:T(8,128)(2,1)} %param.11), kind=kOutput, calls=%fused_computation.19 | convolution fusion | flops 103079215104 | bytes 130023424 | tf_op jit(solution)/shard_map/dot_general | solution.py:26
  420.4 116.4 %add_convert_fusion = bf16[2048,8192]{1,0:T(8,128)(2,1)} fusion(f32[2048,8192]{1,0:T(8,128)} %fusion.9, bf16[8192,3072]{1,0:T(8,128)(2,1)} %param.12, bf16[2048,3072]{1,0:T(8,128)(2,1)} %multiply_convert_fusion.7), kind=kOutput, calls=%fused_computation | convolution fusion | flops 103112769536 | bytes 163577856 | tf_op jit(solution)/shard_map/dot_general | solution.py:27
  536.8 0.0 reduce-scatter.2.cloned.1.call-update
  536.8 0.0 all-gather.5.cloned.1.call-done
  536.8 114.6 %convert_bitcast_fusion.1 = bf16[8192,3072]{0,1:T(8,128)(2,1)} fusion(bf16[2048,3072]{1,0:T(8,128)(2,1)} %get-tuple-element.8, bf16[2048,8192]{1,0:T(8,128)(2,1)} %all-gather.5.cloned.1.call-done), kind=kOutput, calls=%fused_computation.2 | convolution fusion | flops 103104380928 | bytes 96468992 | tf_op jit(solution)/shard_map/dot_general | solution.py:30
  651.5 64.5 %copy.11 = bf16[8192,3072]{1,0:T(8,128)(2,1)} copy(bf16[8192,3072]{0,1:T(8,128)(2,1)} %convert_bitcast_fusion.1) | data formatting | bytes 100663296
  716.0 124.5 %convert_bitcast_fusion = bf16[8192,3072]{0,1:T(8,128)(2,1)} fusion(bf16[2048,8192]{1,0:T(8,128)(2,1)} %all-gather.5.cloned.1.call-done, f32[2048,3072]{1,0:T(8,128)} %get-tuple-element.9, bf16[2048,3072]{1,0:T(8,128)(2,1)} %param.9), kind=kOutput, calls=%fused_computation.1 | convolution fusion | flops 103148421120 | bytes 121634816 | tf_op jit(solution)/shard_map/dot_general | solution.py:31
  840.5 64.5 %copy.12 = bf16[8192,3072]{1,0:T(8,128)(2,1)} copy(bf16[8192,3072]{0,1:T(8,128)(2,1)} %convert_bitcast_fusion) | data formatting | bytes 100663296
  905.0 126.7 %convolution_convert_fusion = bf16[3072,8192]{1,0:T(8,128)(2,1)} fusion(bf16[2048,8192]{1,0:T(8,128)(2,1)} %all-gather.3.cloned.1.call-done, bf16[2048,3072]{1,0:T(8,128)(2,1)} %param.10, bf16[2048,3072]{1,0:T(8,128)(2,1)} %param.9), kind=kOutput, calls=%fused_computation.3 | convolution fusion | flops 103154712576 | bytes 109051904 | tf_op jit(solution)/shard_map/dot_general | solution.py:29
  1031.7 0.0 reduce-scatter.2.cloned.1.call-done
Async XLA Ops:
  7.2 136.7 %all-gather.3.cloned.1.call-start = ((), (), s32[]{:S(2)}) async-start(), calls=%async_computation.1 | async-start | bytes 35651584 | tf_op jit(solution)/shard_map/all_gather | solution.py:19
  7.9 528.9 %all-gather.5.cloned.1.call-start = ((), (), s32[]{:S(2)}) async-start(), calls=%async_computation.3 | async-start | bytes 35651584 | tf_op jit(solution)/shard_map/all_gather | solution.py:20
  8.6 1023.1 %reduce-scatter.2.cloned.1.call-start = ((), (), s32[]{:S(2)}) async-start(), calls=%async_computation.2 | async-start | bytes 35651584 | tf_op jit(solution)/shard_map/reduce_scatter | solution.py:28
Sparse Core Ops, SparseCore 0:
  10.2 133.5 all-gather.2
  146.1 131.2 all-gather.4
  536.9 344.8 reduce-scatter.1

commit v2 on v0

v2 whole, which is shorter than its diff:
```python
import jax
import jax.numpy as jnp
from jax import lax
from jax.experimental import pallas as pl
from jax.experimental.pallas import tpu as pltpu
from jax.sharding import PartitionSpec as P

f32, bf16 = jnp.float32, jnp.bfloat16
NT = (((1,), (1,)), ((), ()))
TN = (((0,), (0,)), ((), ()))

PART = (48, 48, 32)
FROM = (0, 48, 96)
AXES = ((0, 1, 2), (1, 2, 0), (2, 0, 1))
FLIPS = ((0, 0, 0), (1, 0, 0), (0, 1, 0), (0, 0, 1), (1, 1, 0), (1, 0, 1), (0, 1, 1), (1, 1, 1))
HOP = (None, (0, 0), (0, 1), (0, 2), (1, 1), (1, 2), (2, 2), (4, 2))
ROWS = 256


def slot(j, p, k):
    return pl.ds(j * ROWS + 2 * FROM[p] + k * PART[p], PART[p])


def act_grads(g, u, dh):
    s = lax.logistic(g)
    silu = g * s
    return silu * u, (dh * u) * (s + silu * (1.0 - s)), dh * silu


B1, B2, WIDE = 512, 512, 2048


def front(nd, T, D, F):
    n1, n2 = F // B1, D // B2
    steps = 4 * n1 + 3 * n2
    big = 3 * ROWS
    A1, A2 = 2 * n1, 3 * n1 + n2
    dy_at = {1: n1 - 1, 2: n1 + 4, 3: A1 + 3, 4: A1 + 8, 5: A1 + 12, 6: A1 + n2, 7: A1 + n2 + 2}
    x_at = {1: A2 - 1, 2: A2 + 2, 3: A2 + 5, 4: A2 + 8, 5: A2 + 11, 6: A2 + 14, 7: A2 + n2 + 1}

    def kern(x, dy, gate, up, wd, wg, wu, dyr, xr, hid, dg, du, dx,
             dyv, wv, gv, uv, dhv, gu, hv, dxv, send, recv, send2, recv2, ls, gs, ws, hs, xs):
        i = pl.program_id(0)
        me = lax.axis_index("tp")
        at = (me // 8, me // 4 % 2, me // 2 % 2)
        core = me % 2

        def device(flip, k=0):
            c = [1 - at[a] if flip[a] else at[a] for a in range(3)]
            return ((c[0] * 2 + c[1]) * 2 + c[2]) * 2 + (1 - core if k else core)

        def axis_flip(p, bits):
            flip = [0, 0, 0]
            for a, b in zip(AXES[p], bits):
                flip[a] = b
            return flip

        def copy(src, dst, sem):
            return pltpu.make_async_copy(src, dst, sem)

        full, own = (dyr, xr), (dy, x)

        def hop(a, j, p):
            src, along = HOP[j]
            ref = own[a].at[pl.ds(FROM[p], PART[p])] if src == 0 else full[a].at[slot(src, p, 0)]
            bits = [int(b == along) for b in range(3)]
            return pltpu.make_async_remote_copy(
                ref, full[a].at[slot(j, p, 0)], send.at[a, j, p], recv.at[a, j, p],
                device_id={"tp": device(axis_flip(p, bits))}, device_id_type=pl.DeviceIdType.MESH)

        def across(a, j, p):
            ref = own[a].at[pl.ds(FROM[p], PART[p])] if j == 0 else full[a].at[slot(j, p, 0)]
            return pltpu.make_async_remote_copy(
                ref, full[a].at[slot(j, p, 1)], send2.at[a, j, p], recv2.at[a, j, p],
                device_id={"tp": device((0, 0, 0), 1)}, device_id_type=pl.DeviceIdType.MESH)

        def begin(a):
            for p in range(3):
                across(a, 0, p).start()
            for j in (1, 2, 3):
                for p in range(3):
                    hop(a, j, p).start()

        def arrive(a, j):
            for p in range(3):
                hop(a, j, p).wait_recv()
            for later in range(4, 8):
                if HOP[later][0] == j:
                    for p in range(3):
                        hop(a, later, p).start()
            for p in range(3):
                across(a, j, p).start()

        def arrived(a, j):
            for p in range(3):
                across(a, j, p).wait_recv()

        def wdc(j, s):
            return [copy(wd.at[pl.ds(pl.multiple_of(j * B1, B1), B1)], wv.at[s], ws.at[s, 0])]

        def wgu(j, s):
            r = pl.ds(pl.multiple_of(j * B2, B2), B2)
            return [copy(w.at[r], wv.at[s, :, pl.ds(n * F, F)], ws.at[s, n]) for n, w in ((0, wg), (1, wu))]

        def kept(j, row):
            out = []
            for p in range(3):
                for k in range(2):
                    r = pl.ds(pl.multiple_of(device(axis_flip(p, FLIPS[j]), k) * 128 + FROM[p], 16), PART[p])
                    d = pl.ds(row + 2 * FROM[p] + k * PART[p], PART[p])
                    out += [copy(gate.at[r], gv.at[d], gs.at[0, row // ROWS]), copy(up.at[r], uv.at[d], gs.at[1, row // ROWS])]
            return out

        def kept_wait(row):
            d = pl.ds(row, ROWS)
            copy(gate.at[pl.ds(0, ROWS)], gv.at[d], gs.at[0, row // ROWS]).wait()
            copy(up.at[pl.ds(0, ROWS)], uv.at[d], gs.at[1, row // ROWS]).wait()

        def start(cs):
            for c in cs:
                c.start()

        def wait(cs):
            for c in cs:
                c.wait()

        def other(j):
            return [copy(dyr.at[slot(j, p, 1)], dyv.at[slot(j, p, 1)], ls.at[4 + p]) for p in range(3)]

        def load(j, n, row):
            return copy(dyr.at[pl.ds(j * ROWS, n * ROWS)], dyv.at[pl.ds(row, n * ROWS)], ls.at[0])

        def act(row, m, t, s, q):
            w = B1 // 2
            c = pl.ds(pl.multiple_of(t * B1 + q * w, w), w)
            r = pl.ds(row, m)
            h, g, u = act_grads(gv[r, c].astype(f32), uv[r, c].astype(f32), dhv[:m, q * w : (q + 1) * w])
            hv[s, :m, q * w : (q + 1) * w] = h.astype(bf16)
            gu[r, c] = g.astype(bf16)
            gu[r, pl.ds(pl.multiple_of(F + t * B1 + q * w, w), w)] = u.astype(bf16)

        def put_at(to, m, row, t, s):
            r, v, c = pl.ds(to, m), pl.ds(row, m), pl.ds(pl.multiple_of(t * B1, B1), B1)
            c2 = pl.ds(pl.multiple_of(F + t * B1, B1), B1)
            return [copy(hv.at[s, pl.ds(0, m)], hid.at[r, c], hs.at[s, 0]),
                    copy(gu.at[v, c], dg.at[r, c], hs.at[s, 1]),
                    copy(gu.at[v, c2], du.at[r, c], hs.at[s, 2])]

        def put_dx(j, n, t, s):
            out = []
            for b in range(n):
                for p in range(3):
                    for k in range(2):
                        r = pl.ds(pl.multiple_of(device(axis_flip(p, FLIPS[j + b]), k) * 128 + FROM[p], 16), PART[p])
                        v = pl.ds(b * ROWS + 2 * FROM[p] + k * PART[p], PART[p])
                        out.append(copy(dxv.at[s, v], dx.at[r, pl.ds(pl.multiple_of(t * WIDE, WIDE), WIDE)], xs.at[s]))
            return out

        def put_dx_wait(n, s):
            v = pl.ds(0, n * ROWS)
            copy(dxv.at[s, v], dx.at[v, pl.ds(0, WIDE)], xs.at[s]).wait()

        sl = lax.rem(i, 2)
        nx = 1 - sl

        events = {}

        def once(step):
            def add(f):
                events.setdefault(step, []).append(f)
            return add

        def dispatch(at):
            if len(at) == 1:
                @pl.when(i == at[0])
                def _():
                    for f in events[at[0]]:
                        f()
            else:
                mid = len(at) // 2

                @pl.when(i < at[mid])
                def _():
                    dispatch(at[:mid])

                @pl.when(i >= at[mid])
                def _():
                    dispatch(at[mid:])

        @once(0)
        def _():
            start(wdc(0, 0))
            for p in range(3):
                copy(dy.at[pl.ds(FROM[p], PART[p])], dyv.at[slot(0, p, 0)], ls.at[1 + p]).start()
            barrier = pltpu.get_barrier_semaphore()
            peers = [device((1, 0, 0)), device((0, 1, 0)), device((0, 0, 1)), device((0, 0, 0), 1)]
            for d in peers:
                pl.semaphore_signal(barrier, 1, device_id={"tp": d}, device_id_type=pl.DeviceIdType.MESH)
            pl.semaphore_wait(barrier, 4)
            begin(0)
            start(kept(0, 0))
            for p in range(3):
                copy(dy.at[pl.ds(FROM[p], PART[p])], dyv.at[slot(0, p, 0)], ls.at[1 + p]).wait()
                copy(dyv.at[slot(0, p, 0)], dyr.at[slot(0, p, 0)], ls.at[1 + p]).start()
            arrived(0, 0)
            start(other(0))
            wait(other(0))
            kept_wait(0)

        @once(1)
        def _():
            start(kept(1, ROWS))
            for p in range(3):
                copy(dyv.at[slot(0, p, 0)], dyr.at[slot(0, p, 0)], ls.at[1 + p]).wait()
            for p in range(3):
                copy(x.at[pl.ds(FROM[p], PART[p])], dyv.at[pl.ds(2 * ROWS + FROM[p], PART[p])], ls.at[1 + p]).start()

        @once(3)
        def _():
            for p in range(3):
                copy(x.at[pl.ds(FROM[p], PART[p])], dyv.at[pl.ds(2 * ROWS + FROM[p], PART[p])], ls.at[1 + p]).wait()
            for p in range(3):
                copy(dyv.at[pl.ds(2 * ROWS + FROM[p], PART[p])], xr.at[slot(0, p, 0)], ls.at[1 + p]).start()

        @once(n1 - 2)
        def _():
            for p in range(3):
                copy(dyv.at[pl.ds(2 * ROWS + FROM[p], PART[p])], xr.at[slot(0, p, 0)], ls.at[1 + p]).wait()

        def on_arrival(a, j):
            @once((dy_at, x_at)[a][j])
            def _():
                arrive(a, j)
                if (a, j) == (0, 1):
                    for p in range(3):
                        copy(dyr.at[slot(1, p, 0)], dyv.at[slot(1, p, 0)], ls.at[1 + p]).start()
                if (a, j) == (0, 4):
                    begin(1)

        for j in range(1, 8):
            on_arrival(0, j)
            on_arrival(1, j)

        @once(n1)
        def _():
            arrived(0, 1)
            start(other(1))
            kept_wait(ROWS)
            for p in range(3):
                copy(dyr.at[slot(1, p, 0)], dyv.at[slot(1, p, 0)], ls.at[1 + p]).wait()
            wait(other(1))

        def next_rows(s0, j0):
            for b in range(3):
                once(s0 + 1 + b)(lambda b=b: start(kept(j0 + b, b * ROWS)))

            @once(s0 + n2 - 4)
            def _():
                for b in range(3):
                    arrived(0, j0 + b)
                load(j0, 3, 0).start()

            @once(s0 + n2)
            def _():
                for b in range(3):
                    kept_wait(b * ROWS)
                load(j0, 3, 0).wait()

        next_rows(A1, 2)
        next_rows(A2, 5)
        dispatch(sorted(events))

        per = WIDE // B2

        def dh_step(m, row, t, prev_row, prev_t):
            wait(wdc(t, sl))
            for q in range(2):
                w = B1 // 2
                act(prev_row, m, prev_t, sl, q)
                dhv[:m, q * w : (q + 1) * w] = lax.dot_general(
                    dyv[pl.ds(row, m)], wv[sl, q * w : (q + 1) * w], NT, preferred_element_type=f32)

        def put_small(start_if, wait_if):
            @pl.when(wait_if)
            def _():
                u = i - 3
                b = u // n1
                wait(put_at(b * ROWS, ROWS, b * ROWS, u - b * n1, sl))

            @pl.when(start_if)
            def _():
                u = i - 2
                b = u // n1
                start(put_at(b * ROWS, ROWS, b * ROWS, u - b * n1, nx))

        def dx_step(m, t):
            wait(wgu(t, sl))
            dxv[t // per % 2, :m, pl.ds(pl.multiple_of(t % per * B2, B2), B2)] = lax.dot_general(
                gu[:m], wv[sl, :, : 2 * F], NT, preferred_element_type=f32).astype(bf16)

        @pl.when(i < 2 * n1)
        def _():
            t = i % n1

            @pl.when(i < 2 * n1 - 1)
            def _():
                start(wdc((i + 1) % n1, nx))

            @pl.when(i == 2 * n1 - 1)
            def _():
                start(wgu(0, nx))

            put_small(i >= 2, i >= 3)
            prev = jnp.maximum(i - 1, 0)
            dh_step(ROWS, pl.multiple_of(i // n1 * ROWS, ROWS), t, pl.multiple_of(prev // n1 * ROWS, ROWS), prev % n1)

        @pl.when((i >= A1) & (i < A1 + n2))
        def _():
            t = i - A1

            @pl.when(t < n2 - 1)
            def _():
                start(wgu(t + 1, nx))

            @pl.when(t == n2 - 1)
            def _():
                start(wdc(0, nx))

            @pl.when(t < 3)
            def _():
                put_small(t < 2, t < 3)

                @pl.when(t == 0)
                def _():
                    for q in range(2):
                        act(ROWS, ROWS, n1 - 1, sl, q)

            @pl.when((t >= per) & (t % per == 0))
            def _():
                start(put_dx(0, 2, t // per - 1, (t // per - 1) % 2))

                @pl.when(t >= 2 * per)
                def _():
                    put_dx_wait(2, t // per % 2)

            dx_step(2 * ROWS, t)

        @pl.when(i >= A1 + n2)
        def _():
            second = i >= A2 + n2
            k = i - jnp.where(second, A2 + n2, A1 + n2)
            j0 = jnp.where(second, 5 * ROWS, 2 * ROWS)

            @pl.when((k < n1 - 1) | ((k == n1 + n2 - 1) & (i < steps - 1)))
            def _():
                start(wdc(jnp.where(k < n1 - 1, k + 1, 0), nx))

            @pl.when((k >= n1 - 1) & (k < n1 + n2 - 1))
            def _():
                start(wgu(k + 1 - n1, nx))

            @pl.when((k >= 2) & (k < n1 + 3))
            def _():
                @pl.when(k >= 3)
                def _():
                    wait(put_at(pl.multiple_of(j0, ROWS), big, 0, k - 3, sl))

                @pl.when(k < n1 + 2)
                def _():
                    start(put_at(pl.multiple_of(j0, ROWS), big, 0, k - 2, nx))

            @pl.when(k < n1)
            def _():
                @pl.when(jnp.logical_not(second) & (k % per == 0) & (k <= per))
                def _():
                    last = n2 // per - 1

                    @pl.when(k == 0)
                    def _():
                        start(put_dx(0, 2, last, last % 2))
                        put_dx_wait(2, (last - 1) % 2)

                    @pl.when(k == per)
                    def _():
                        put_dx_wait(2, last % 2)

                @pl.when(second & (k % per == 0) & (k <= per))
                def _():
                    last = n2 // per - 1

                    @pl.when(k == 0)
                    def _():
                        start(put_dx(2, 3, last, last % 2))
                        put_dx_wait(3, (last - 1) % 2)

                    @pl.when(k == per)
                    def _():
                        put_dx_wait(3, last % 2)

                dh_step(big, 0, k, 0, jnp.maximum(k - 1, 0))

            @pl.when(k >= n1)
            def _():
                t = k - n1

                @pl.when(t == 0)
                def _():
                    for q in range(2):
                        act(0, big, n1 - 1, sl, q)

                @pl.when((t >= per) & (t % per == 0))
                def _():
                    g = t // per

                    @pl.when(second)
                    def _():
                        start(put_dx(5, 3, g - 1, (g - 1) % 2))

                    @pl.when(jnp.logical_not(second))
                    def _():
                        start(put_dx(2, 3, g - 1, (g - 1) % 2))

                    @pl.when(t >= 2 * per)
                    def _():
                        put_dx_wait(3, g % 2)

                dx_step(big, t)

        @pl.when(i == steps - 1)
        def _():
            last = n2 // per - 1
            start(put_dx(5, 3, last, last % 2))
            put_dx_wait(3, (last - 1) % 2)
            put_dx_wait(3, last % 2)
            for a in range(2):
                for j in range(8):
                    for p in range(3):
                        across(a, j, p).wait_send()
                        if j:
                            hop(a, j, p).wait_send()
            for j in range(8):
                arrived(1, j)

    sh = jax.ShapeDtypeStruct
    anyspec = pl.BlockSpec(memory_space=pl.ANY)
    dma = pltpu.SemaphoreType.DMA
    return pl.pallas_call(
        kern, grid=(steps,), name="front", in_specs=[anyspec] * 7, out_specs=[anyspec] * 6,
        out_shape=[sh((T, D), bf16)] * 2 + [sh((T, F), bf16)] * 3 + [sh((T, D), bf16)],
        scratch_shapes=[
            pltpu.VMEM((big, D), bf16), pltpu.VMEM((2, B1, D), bf16), pltpu.VMEM((big, F), bf16), pltpu.VMEM((big, F), bf16),
            pltpu.VMEM((big, B1), f32), pltpu.VMEM((big, 2 * F), bf16), pltpu.VMEM((2, big, B1), bf16),
            pltpu.VMEM((2, big, WIDE), bf16),
            dma((2, 8, 3)), dma((2, 8, 3)), dma((2, 8, 3)), dma((2, 8, 3)), dma((7,)), dma((2, 3)), dma((2, 2)), dma((2, 3)), dma((2,)),
        ],
        compiler_params=pltpu.CompilerParams(
            vmem_limit_bytes=62 * 2**20, dimension_semantics=("arbitrary",), collective_id=0, has_side_effects=True),
        cost_estimate=pl.CostEstimate(flops=6 * T * D * F, bytes_accessed=2 * (9 * D * F + 6 * T * D + 5 * T * F), transcendentals=T * F),
    )


def weights(T, D, F, bw=512, mt=768):
    n = D // bw

    def kern(dy, x, hid, dg, du, dwd, dwg, dwu, hv, gv, uv, blk, ws, bs):
        i = pl.program_id(0)

        def block(a, j, s):
            return pltpu.make_async_copy(a.at[:, pl.ds(pl.multiple_of(j * bw, bw), bw)], blk.at[s], bs.at[s])

        def whole(k):
            return pltpu.make_async_copy((hid, dg, du)[k], (hv, gv, uv)[k], ws.at[k])

        s = lax.rem(i, 2)

        @pl.when(i == 0)
        def _():
            block(dy, 0, 0).start()
            whole(0).start()
            whole(0).wait()

        @pl.when(i + 1 < n)
        def _():
            block(dy, i + 1, 1 - s).start()

        @pl.when((i + 1 >= n) & (i + 1 < 2 * n))
        def _():
            block(x, i + 1 - n, 1 - s).start()

        @pl.when(i == 1)
        def _():
            whole(1).start()
            whole(2).start()

        @pl.when(i < n)
        def _():
            block(dy, i, s).wait()
            for m in range(0, F, mt):
                dwd[m : m + mt, :] = lax.dot_general(
                    hv[:, m : m + mt], blk[s], TN, preferred_element_type=f32).astype(bf16)

        @pl.when(i == n)
        def _():
            whole(1).wait()
            whole(2).wait()

        @pl.when(i >= n)
        def _():
            block(x, i - n, s).wait()
            for src, dst in ((gv, dwg), (uv, dwu)):
                for m in range(0, F, mt):
                    dst[:, m : m + mt] = lax.dot_general(
                        blk[s], src[:, m : m + mt], TN, preferred_element_type=f32).astype(bf16)

    sh = jax.ShapeDtypeStruct
    dma = pltpu.SemaphoreType.DMA
    late = pl.BlockSpec((bw, F), lambda i: (jnp.maximum(i - n, 0), 0))
    return pl.pallas_call(
        kern, grid=(2 * n,), name="weights", in_specs=[pl.BlockSpec(memory_space=pl.ANY)] * 5,
        out_specs=[pl.BlockSpec((F, bw), lambda i: (0, jnp.minimum(i, n - 1))), late, late],
        out_shape=[sh((F, D), bf16), sh((D, F), bf16), sh((D, F), bf16)],
        scratch_shapes=[pltpu.VMEM((T, F), bf16)] * 3 + [pltpu.VMEM((2, T, bw), bf16), dma((3,)), dma((2,))],
        compiler_params=pltpu.CompilerParams(vmem_limit_bytes=62 * 2**20, dimension_semantics=("arbitrary",)),
        cost_estimate=pl.CostEstimate(flops=6 * T * D * F, bytes_accessed=2 * (3 * D * F + 2 * T * D + 3 * T * F), transcendentals=0),
    )


def solution(mesh):
    rows, cols = P(("dp", "tp"), None), P("dp", "tp")
    wcol, wrow = P(None, "tp"), P("tp", None)
    nd = mesh.shape["tp"]

    def body(x, dy, gate, up, w_gate, w_up, w_down):
        T, F, D = gate.shape[0], gate.shape[1], x.shape[1]
        dyr, xr, hid, dg, du, dx = front(nd, T, D, F)(x, dy, gate, up, w_down, w_gate, w_up)
        dx = lax.psum_scatter(dx, "tp", scatter_dimension=0, tiled=True)
        dwd, dwg, dwu = weights(T, D, F)(dyr, xr, hid, dg, du)
        return dx, dwg, dwu, dwd

    return jax.shard_map(
        body, mesh=mesh, in_specs=(rows, rows, cols, cols, wcol, wcol, wrow), out_specs=(rows, cols, cols, rows), check_vma=False)
```

time: 1700 us -> 740 us (0.44)
  matrix products: 836 us -> 0 us
  Pallas kernels: 0 us -> 709 us
  waiting for transfers between devices: 540 us -> 17.4 us
  local copies, waits for them, and re-layouts: 135 us -> 0 us
  other arithmetic: 128 us -> 0 us
  starting transfers between devices: 37.3 us -> 0.04 us
    dot_general x20 -> x0, matrix products: 836 us -> none  [the longest x3 356 us: by_group(): jnp.einsum('gta,gtb->gab', a, b, preferred_element_type=jnp.float32)]
    pallas_call x0 -> x2, Pallas kernels: none -> 709 us  [the longest x1 380 us: body(): front(nd, T, D, F)(x, dy, gate, up, w_down, w_gate, w_up)]
    dot_general x34 -> x0, waiting for transfers between devices: 404 us -> none  [step(): dx = jnp.dot(d_gate, w_gate.T) + jnp.dot(d_up, w_up.T)]
    unnamed x4 -> x1, waiting for transfers between devices: 137 us -> 0.02 us
    unnamed x8 -> x0, local copies, waits for them, and re-layouts: 129 us -> none
    dot_general x32 -> x0, other arithmetic: 123 us -> none  [the longest x16 89.5 us: step(): dx = jnp.dot(d_gate, w_gate.T) + jnp.dot(d_up, w_up.T)]
    dot_general x34 -> x0, starting transfers between devices: 37.2 us -> none  [step(): dx = jnp.dot(d_gate, w_gate.T) + jnp.dot(d_up, w_up.T)]
    reduce_scatter x0 -> x1, waiting for transfers between devices: none -> 17.4 us  [body(): dx = lax.psum_scatter(dx, 'tp', scatter_dimension=0, tiled=True)]
  transfers between devices with their start and end apart: 36 -> 1, of which waited for: 19 -> 1; matrix products, arithmetic and copies ran while one was open for 64% -> 0% of each run, Pallas kernels for 0% -> 44%
where the time goes in v2:
time: 740 us
  Pallas kernels  709 us (96%)
  waiting for transfers between devices  17.4 us (2%)
  between operations  14 us (2%)
    pallas_call x1, Pallas kernels, body(): front(nd, T, D, F)(x, dy, gate, up, w_down, w_gate, w_up)  380 us
    pallas_call x1, Pallas kernels, body(): dwd, dwg, dwu = weights(T, D, F)(dyr, xr, hid, dg, du)  328 us
    reduce_scatter x1, waiting for transfers between devices, body(): dx = lax.psum_scatter(dx, 'tp', scatter_dimension=0, tiled=True)  17.4 us
  transfers between devices with their start and end apart: 1, of which 1 were waited for; matrix products, arithmetic and copies ran while one was open for 0% of the time, Pallas kernels for 44%

profile of v2, /device:TPU:1, one launch (start us, length us, event | category | flops | bytes accessed | tf_op | source)
XLA Modules:
  0.0 740.1 jit_solution(14294781548193321237)
XLA Ops:
  7.2 0.0 reduce-scatter.2.cloned.1.call-start
  7.2 380.3 %front.1 = (bf16[2048,8192]{1,0:T(8,128)(2,1)}, bf16[2048,8192]{1,0:T(8,128)(2,1)}, bf16[2048,3072]{1,0:T(8,128)(2,1)}, bf16[2048,3072]{1,0:T(8,128)(2,1)}, bf16...) custom-call(bf16[128,8192]{1,0:T(8,128)(2,1)} %x.1, bf16[128,8192]{1,0:T(8,128)(2,1)} %dy.1, bf16[2048,3072]{1,0:T(8,128)(2,1)} %gate.1, ...), custom_call_target="tpu_custom_call" | custom-call | flops 309237645312 | bytes 717225984 | tf_op jit(solution)/shard_map/front/pallas_call | solution.py:535
  387.5 0.0 reduce-scatter.2.cloned.1.call-update
  387.5 328.3 %weights.1 = (bf16[3072,8192]{1,0:T(8,128)(2,1)}, bf16[8192,3072]{1,0:T(8,128)(2,1)}, bf16[8192,3072]{1,0:T(8,128)(2,1)}) custom-call(bf16[2048,8192]{1,0:T(8,128)(2,1)} %get-tuple-element.14.dy, bf16[2048,8192]{1,0:T(8,128)(2,1)} %get-tuple-element.15.x, bf16[2048,3072]{1,0:T(8,128)(2,1)} %get-tuple-element.16.hid, ...), custom_call_target="tpu_custom_call" | custom-call | flops 309237645312 | bytes 255852544 | tf_op jit(solution)/shard_map/weights/pallas_call | solution.py:537
  715.9 17.4 %reduce-scatter.2.cloned.1.call-done = bf16[128,8192]{1,0:T(8,128)(2,1)} async-done(((bf16[2048,8192]{1,0:T(8,128)(2,1)}), bf16[128,8192]{1,0:T(8,128)(2,1)}) %reduce-scatter.2.cloned.1.call-update) | async-done | bytes 2097168 | tf_op jit(solution)/shard_map/reduce_scatter | solution.py:536
Async XLA Ops:
  7.2 726.1 %reduce-scatter.2.cloned.1.call-start = ((), (), s32[]{:S(2)}) async-start(), calls=%async_computation.1 | async-start | bytes 35651584 | tf_op jit(solution)/shard_map/reduce_scatter | solution.py:536
Sparse Core Ops, SparseCore 0:
  387.7 345.5 reduce-scatter.1

commit v3 on v2

--- a/solution.py
+++ b/solution.py
@@ -27,7 +27,7 @@
     return silu * u, (dh * u) * (s + silu * (1.0 - s)), dh * silu
 
 
-B1, B2, WIDE = 512, 512, 2048
+B1, B2, WIDE = 512, 1024, 1024
 
 
 def front(nd, T, D, F):
@@ -35,8 +35,8 @@
     steps = 4 * n1 + 3 * n2
     big = 3 * ROWS
     A1, A2 = 2 * n1, 3 * n1 + n2
-    dy_at = {1: n1 - 1, 2: n1 + 4, 3: A1 + 3, 4: A1 + 8, 5: A1 + 12, 6: A1 + n2, 7: A1 + n2 + 2}
-    x_at = {1: A2 - 1, 2: A2 + 2, 3: A2 + 5, 4: A2 + 8, 5: A2 + 11, 6: A2 + 14, 7: A2 + n2 + 1}
+    dy_at = {1: n1 - 1, 2: n1 + 5, 3: A1 + 3, 4: A1 + 5, 5: A1 + n2, 6: A1 + n2 + 2, 7: A1 + n2 + 5}
+    x_at = {1: A2 + 1, 2: A2 + 3, 3: A2 + 4, 4: A2 + 6, 5: A2 + 7, 6: A2 + 9, 7: A2 + 12}
 
     def kern(x, dy, gate, up, wd, wg, wu, dyr, xr, hid, dg, du, dx,
              dyv, wv, gv, uv, dhv, gu, hv, dxv, send, recv, send2, recv2, ls, gs, ws, hs, xs):
@@ -96,7 +96,9 @@
                 across(a, j, p).wait_recv()
 
         def wdc(j, s):
-            return [copy(wd.at[pl.ds(pl.multiple_of(j * B1, B1), B1)], wv.at[s], ws.at[s, 0])]
+            r = pl.ds(pl.multiple_of(j * B1, B1), B1)
+            return [copy(wd.at[r, pl.ds(h * D // 2, D // 2)], wv.at[s, pl.ds(h * B1, B1), pl.ds(0, D // 2)], ws.at[s, h])
+                    for h in range(2)]
 
         def wgu(j, s):
             r = pl.ds(pl.multiple_of(j * B2, B2), B2)
@@ -133,11 +135,12 @@
         def act(row, m, t, s, q):
             w = B1 // 2
             c = pl.ds(pl.multiple_of(t * B1 + q * w, w), w)
-            r = pl.ds(row, m)
-            h, g, u = act_grads(gv[r, c].astype(f32), uv[r, c].astype(f32), dhv[:m, q * w : (q + 1) * w])
-            hv[s, :m, q * w : (q + 1) * w] = h.astype(bf16)
-            gu[r, c] = g.astype(bf16)
-            gu[r, pl.ds(pl.multiple_of(F + t * B1 + q * w, w), w)] = u.astype(bf16)
+            for o in range(0, m, 128):
+                r = pl.ds(row + o, 128)
+                h, g, u = act_grads(gv[r, c].astype(f32), uv[r, c].astype(f32), dhv[o : o + 128, q * w : (q + 1) * w])
+                hv[s, o : o + 128, q * w : (q + 1) * w] = h.astype(bf16)
+                gu[r, c] = g.astype(bf16)
+                gu[r, pl.ds(pl.multiple_of(F + t * B1 + q * w, w), w)] = u.astype(bf16)
 
         def put_at(to, m, row, t, s):
             r, v, c = pl.ds(to, m), pl.ds(row, m), pl.ds(pl.multiple_of(t * B1, B1), B1)
@@ -254,7 +257,7 @@
             for b in range(3):
                 once(s0 + 1 + b)(lambda b=b: start(kept(j0 + b, b * ROWS)))
 
-            @once(s0 + n2 - 4)
+            @once(s0 + n2 - 1)
             def _():
                 for b in range(3):
                     arrived(0, j0 + b)
@@ -274,11 +277,14 @@
 
         def dh_step(m, row, t, prev_row, prev_t):
             wait(wdc(t, sl))
-            for q in range(2):
-                w = B1 // 2
-                act(prev_row, m, prev_t, sl, q)
-                dhv[:m, q * w : (q + 1) * w] = lax.dot_general(
-                    dyv[pl.ds(row, m)], wv[sl, q * w : (q + 1) * w], NT, preferred_element_type=f32)
+            r, h = pl.ds(row, m), D // 2
+            w = B1 if m == ROWS else B1 // 2
+            for q in range(0, B1, w):
+                for o in range(q, q + w, B1 // 2):
+                    act(prev_row, m, prev_t, sl, o // (B1 // 2))
+                dhv[:m, q : q + w] = lax.dot_general(
+                    dyv[r, :h], wv[sl, q : q + w, :h], NT, preferred_element_type=f32
+                ) + lax.dot_general(dyv[r, h:], wv[sl, B1 + q : B1 + q + w, :h], NT, preferred_element_type=f32)
 
         def put_small(start_if, wait_if):
             @pl.when(wait_if)
@@ -295,8 +301,16 @@
 
         def dx_step(m, t):
             wait(wgu(t, sl))
-            dxv[t // per % 2, :m, pl.ds(pl.multiple_of(t % per * B2, B2), B2)] = lax.dot_general(
-                gu[:m], wv[sl, :, : 2 * F], NT, preferred_element_type=f32).astype(bf16)
+            if m == big:
+                for q in range(0, B2, B2 // 4):
+                    dxv[t % 2, :, q : q + B2 // 4] = lax.dot_general(
+                        gu[...], wv[sl, q : q + B2 // 4], NT, preferred_element_type=f32).astype(bf16)
+            else:
+                def part(q, _):
+                    c = pl.ds(pl.multiple_of(q * 512, 512), 512)
+                    dxv[t % 2, :m, c] = lax.dot_general(gu[:m], wv[sl, c], NT, preferred_element_type=f32).astype(bf16)
+                    return 0
+                lax.fori_loop(0, B2 // 512, part, 0)
 
         @pl.when(i < 2 * n1)
         def _():
@@ -448,13 +462,13 @@
         kern, grid=(steps,), name="front", in_specs=[anyspec] * 7, out_specs=[anyspec] * 6,
         out_shape=[sh((T, D), bf16)] * 2 + [sh((T, F), bf16)] * 3 + [sh((T, D), bf16)],
         scratch_shapes=[
-            pltpu.VMEM((big, D), bf16), pltpu.VMEM((2, B1, D), bf16), pltpu.VMEM((big, F), bf16), pltpu.VMEM((big, F), bf16),
+            pltpu.VMEM((big, D), bf16), pltpu.VMEM((2, B2, 2 * F), bf16), pltpu.VMEM((big, F), bf16), pltpu.VMEM((big, F), bf16),
             pltpu.VMEM((big, B1), f32), pltpu.VMEM((big, 2 * F), bf16), pltpu.VMEM((2, big, B1), bf16),
             pltpu.VMEM((2, big, WIDE), bf16),
             dma((2, 8, 3)), dma((2, 8, 3)), dma((2, 8, 3)), dma((2, 8, 3)), dma((7,)), dma((2, 3)), dma((2, 2)), dma((2, 3)), dma((2,)),
         ],
         compiler_params=pltpu.CompilerParams(
-            vmem_limit_bytes=62 * 2**20, dimension_semantics=("arbitrary",), collective_id=0, has_side_effects=True),
+            vmem_limit_bytes=67_043_328, dimension_semantics=("arbitrary",), collective_id=0, has_side_effects=True),
         cost_estimate=pl.CostEstimate(flops=6 * T * D * F, bytes_accessed=2 * (9 * D * F + 6 * T * D + 5 * T * F), transcendentals=T * F),
     )
 
@@ -495,9 +509,14 @@
         @pl.when(i < n)
         def _():
             block(dy, i, s).wait()
-            for m in range(0, F, mt):
-                dwd[m : m + mt, :] = lax.dot_general(
-                    hv[:, m : m + mt], blk[s], TN, preferred_element_type=f32).astype(bf16)
+
+            def part(h, _):
+                for m in range(2):
+                    r = pl.ds(pl.multiple_of((2 * h + m) * mt, mt), mt)
+                    dwd[r, :] = lax.dot_general(hv[:, r], blk[s], TN, preferred_element_type=f32).astype(bf16)
+                return 0
+
+            lax.fori_loop(0, F // mt // 2, part, 0)
 
         @pl.when(i == n)
         def _():
@@ -507,10 +526,15 @@
         @pl.when(i >= n)
         def _():
             block(x, i - n, s).wait()
-            for src, dst in ((gv, dwg), (uv, dwu)):
-                for m in range(0, F, mt):
-                    dst[:, m : m + mt] = lax.dot_general(
-                        blk[s], src[:, m : m + mt], TN, preferred_element_type=f32).astype(bf16)
+
+            def part(h, _):
+                for src, dst in ((gv, dwg), (uv, dwu)):
+                    for m in range(2):
+                        c = pl.ds(pl.multiple_of((2 * h + m) * mt, mt), mt)
+                        dst[:, c] = lax.dot_general(blk[s], src[:, c], TN, preferred_element_type=f32).astype(bf16)
+                return 0
+
+            lax.fori_loop(0, F // mt // 2, part, 0)
 
     sh = jax.ShapeDtypeStruct
     dma = pltpu.SemaphoreType.DMA

time: 740 us -> 731 us (0.988)
  waiting for transfers between devices: 17.4 us -> 5.74 us
    pallas_call x1, Pallas kernels: 328 us -> 340 us  [body(): dwd, dwg, dwu = weights(T, D, F)(dyr, xr, hid, dg, du)]
    reduce_scatter x1, waiting for transfers between devices: 17.4 us -> 5.72 us  [body(): dx = lax.psum_scatter(dx, 'tp', scatter_dimension=0, tiled=True)]
    pallas_call x1, Pallas kernels: 380 us -> 371 us  [body(): front(nd, T, D, F)(x, dy, gate, up, w_down, w_gate, w_up)]
  transfers between devices with their start and end apart: 1 -> 1, of which waited for: 1 -> 1; matrix products, arithmetic and copies ran while one was open for 0% -> 0% of each run, Pallas kernels for 44% -> 46%
where the time goes in v3:
time: 731 us
  Pallas kernels  711 us (97%)
  between operations  14 us (2%)
    pallas_call x1, Pallas kernels, body(): front(nd, T, D, F)(x, dy, gate, up, w_down, w_gate, w_up)  371 us
    pallas_call x1, Pallas kernels, body(): dwd, dwg, dwu = weights(T, D, F)(dyr, xr, hid, dg, du)  340 us
  transfers between devices with their start and end apart: 1, of which 1 were waited for; matrix products, arithmetic and copies ran while one was open for 0% of the time, Pallas kernels for 46%

profile of v3, /device:TPU:1, one launch (start us, length us, event | category | flops | bytes accessed | tf_op | source)
XLA Modules:
  0.0 731.3 jit_solution(6085457616722367624)
XLA Ops:
  7.2 0.0 reduce-scatter.2.cloned.1.call-start
  7.2 371.5 %front.1 = (bf16[2048,8192]{1,0:T(8,128)(2,1)}, bf16[2048,8192]{1,0:T(8,128)(2,1)}, bf16[2048,3072]{1,0:T(8,128)(2,1)}, bf16[2048,3072]{1,0:T(8,128)(2,1)}, bf16...) custom-call(bf16[128,8192]{1,0:T(8,128)(2,1)} %x.1, bf16[128,8192]{1,0:T(8,128)(2,1)} %dy.1, bf16[2048,3072]{1,0:T(8,128)(2,1)} %gate.1, ...), custom_call_target="tpu_custom_call" | custom-call | flops 309237645312 | bytes 717225984 | tf_op jit(solution)/shard_map/front/pallas_call | solution.py:559
  378.7 0.0 reduce-scatter.2.cloned.1.call-update
  378.7 340.0 %weights.1 = (bf16[3072,8192]{1,0:T(8,128)(2,1)}, bf16[8192,3072]{1,0:T(8,128)(2,1)}, bf16[8192,3072]{1,0:T(8,128)(2,1)}) custom-call(bf16[2048,8192]{1,0:T(8,128)(2,1)} %get-tuple-element.14.dy, bf16[2048,8192]{1,0:T(8,128)(2,1)} %get-tuple-element.15.x, bf16[2048,3072]{1,0:T(8,128)(2,1)} %get-tuple-element.16.hid, ...), custom_call_target="tpu_custom_call" | custom-call | flops 309237645312 | bytes 255852544 | tf_op jit(solution)/shard_map/weights/pallas_call | solution.py:561
  718.8 5.7 reduce-scatter.2.cloned.1.call-done
Async XLA Ops:
  7.2 717.3 %reduce-scatter.2.cloned.1.call-start = ((), (), s32[]{:S(2)}) async-start(), calls=%async_computation.1 | async-start | bytes 35651584 | tf_op jit(solution)/shard_map/reduce_scatter | solution.py:560
Sparse Core Ops, SparseCore 0:
  378.8 345.5 reduce-scatter.1
